TPU v7x, 512 devices: a whole 4x4x16 slice. The times are simulated.
512 devices in a mesh: row: 16 (over z), col: 32 (over x, y, core).
Axes of the slice: x: 4, y: 4, z: 16, core: 2. Of those that a mesh axis runs over, the one named last changes fastest.
Arguments:
- rhs_panels: float32 [3, 16, 32, 64, 256], P(None, 'row', 'col'), may hold values from -6 to 6
- inverse_diag: bfloat16 [3, 16, 32, 256, 256], P(None, 'row', 'col'), may hold values from -0.375 to 0.375
- factor_blocks: bfloat16 [3, 16, 320, 256, 256], P(None, 'row', 'col'), may hold values from -0.078125 to 0.078125
- block_target: int32 [3, 16, 320], P(None, 'row', 'col'), may hold values from 0 to 15, as said below
- block_source: int32 [3, 16, 320], P(None, 'row', 'col'), may hold values from 0 to 31, as said below
Outputs:
- solution: float32 [3, 16, 32, 64, 256], P(None, 'row', 'col')
Inputs may be any that keep to these rules, and one draw needn't show every extreme that they name: (block_target[p, r, q] - r) modulo 16 is below 2, or equals 8, or equals 15; each of 1, 8 and 15 occurs. (block_source[p, r, q] - q // 10) modulo 32 is below 2, or equals 16, or equals 31; each of 1, 16 and 31 occurs.
All inputs are finite; a program needn't handle non-finite values.
Results may differ from a plain program's by a relative error of at most 0.014.
Values may be sent and summed in bfloat16 or wider, within the bound.
No kernel may reach another device: no remote copies, remote signals or barrier semaphores. Data moves between devices by JAX's collectives and lax.ppermute only.
A program may use at most 64 MiB of HBM per device.

v0:
```python
import jax
import jax.numpy as jnp
from jax import lax
from jax.sharding import PartitionSpec as P

WINDOW = 2


def from_behind(value, axis, steps):
    count = lax.axis_size(axis)
    pairs = [(source, (source + steps) % count) for source in range(count)]
    return lax.ppermute(value, axis, pairs)


def laid_out(pieces, dim):
    dims = list(pieces.shape[1:])
    dims[dim] *= pieces.shape[0]
    return jnp.moveaxis(pieces, 0, dim).reshape(dims)


def from_everyone(value, axis):
    count = lax.axis_size(axis)
    return lax.all_to_all(
        jnp.broadcast_to(value[None], (count, *value.shape)), axis, 0, 0, tiled=True
    )


def collect(value, axis, dim):
    return laid_out(from_everyone(value, axis), dim)


def pair_table(levels):
    return [
        (target_lvl, source_lvl)
        for target_lvl in range(1, levels)
        for source_lvl in range(target_lvl)
    ]


def offset_choices(window, count):
    values = sorted(set(list(range(window)) + [count // 2, count - 1]))
    return values


def offset_places(offsets, values):
    places = jnp.zeros(offsets.shape, jnp.int32)
    for position, value in enumerate(values):
        places = places + jnp.where(offsets == value, position, 0).astype(jnp.int32)
    return places


def spread_rows(indices, row_count, products):
    onehot = (indices[None, :] == jnp.arange(row_count, dtype=jnp.int32)[:, None]).astype(
        jnp.float32
    )
    flattened = products.reshape(products.shape[0], -1)
    summed = jnp.dot(
        onehot, flattened, precision=lax.Precision.HIGHEST, preferred_element_type=jnp.float32
    )
    return summed.reshape((row_count,) + products.shape[1:])


def deliver_rows(partial_value, values):
    summed = partial_value[0].astype(jnp.bfloat16).astype(jnp.float32)
    for position in range(1, partial_value.shape[0]):
        moved = from_behind(partial_value[position].astype(jnp.bfloat16), "row", values[position])
        summed = summed + moved.astype(jnp.float32)
    return summed


def deliver_cols(partial_value, values):
    summed = partial_value[0].astype(jnp.bfloat16).astype(jnp.float32)
    for position in range(1, partial_value.shape[0]):
        moved = from_behind(partial_value[position].astype(jnp.bfloat16), "col", values[position])
        summed = summed + moved.astype(jnp.float32)
    return summed


def shards(rhs_panels, inverse_diag, factor_blocks, block_target, block_source):
    levels = rhs_panels.shape[0]
    row_devices = lax.axis_size("row")
    col_devices = lax.axis_size("col")
    pair_list = pair_table(levels)
    blocks = factor_blocks[:, 0]
    targets = block_target[:, 0]
    sources = block_source[:, 0]
    row_values = offset_choices(WINDOW, row_devices)
    col_values = offset_choices(WINDOW, col_devices)
    row_keys = offset_places((targets - lax.axis_index("row")) % row_devices, row_values)
    col_keys = offset_places((sources - lax.axis_index("col")) % col_devices, col_values)
    row_width = len(row_values)
    col_width = len(col_values)
    forward = []
    gathered = {}
    for current in range(levels):
        residual = rhs_panels[current, 0, 0]
        if current > 0:
            partial_value = jnp.zeros((row_width,) + residual.shape, jnp.float32)
            for pair_idx, pair_info in enumerate(pair_list):
                if pair_info[0] == current:
                    picked = jnp.take(gathered[pair_info[1]], sources[pair_idx], axis=0)
                    products = jnp.einsum(
                        "snb,sab->sna", picked, blocks[pair_idx], preferred_element_type=jnp.float32
                    )
                    partial_value = partial_value + spread_rows(
                        row_keys[pair_idx], row_width, products
                    )
            summed = deliver_rows(partial_value, row_values)
            residual = residual - summed
        reduced = residual.astype(jnp.bfloat16)
        panel_now = lax.dot_general(
            reduced,
            inverse_diag[current, 0, 0],
            (((1,), (1,)), ((), ())),
            preferred_element_type=jnp.float32,
        )
        forward.append(panel_now)
        if current < levels - 1:
            outgoing = panel_now.astype(jnp.bfloat16)[None]
            gathered[current] = collect(outgoing, "col", 0)
    solutions = [None] * levels
    gathered_back = {}
    for current in reversed(range(levels)):
        residual = forward[current]
        if current < levels - 1:
            partial_value = jnp.zeros((col_width,) + residual.shape, jnp.float32)
            for pair_idx, pair_info in enumerate(pair_list):
                if pair_info[1] == current:
                    picked = jnp.take(gathered_back[pair_info[0]], targets[pair_idx], axis=0)
                    products = jnp.einsum(
                        "snb,sba->sna", picked, blocks[pair_idx], preferred_element_type=jnp.float32
                    )
                    partial_value = partial_value + spread_rows(
                        col_keys[pair_idx], col_width, products
                    )
            summed = deliver_cols(partial_value, col_values)
            residual = residual - summed
        reduced = residual.astype(jnp.bfloat16)
        answer = jnp.dot(reduced, inverse_diag[current, 0, 0], preferred_element_type=jnp.float32)
        solutions[current] = answer
        if current > 0:
            outgoing = answer.astype(jnp.bfloat16)[None]
            gathered_back[current] = lax.all_gather(outgoing, "row", axis=0, tiled=True)
    return jnp.stack(solutions)[:, None, None]


def solution(mesh):
    placed = (
        P(None, "row", "col", None, None),
        P(None, "row", "col", None, None),
        P(None, "row", "col", None, None),
        P(None, "row", "col"),
        P(None, "row", "col"),
    )
    return jax.shard_map(
        shards,
        mesh=mesh,
        in_specs=placed,
        out_specs=P(None, "row", "col", None, None),
        check_vma=False,
    )
```

profile of v0, /device:TPU:32, one launch (start us, length us, event | category | flops | bytes accessed | tf_op | source)
XLA Modules:
  0.0 198.4 jit_solution(18369573394711938383)
XLA Ops:
  2.2 7.3 %all-to-all-start = ((bf16[32,1,64,256]{3,2,1,0:T(8,128)(2,1)}), bf16[32,1,64,256]{3,2,1,0:T(8,128)(2,1)S(1)}, u32[]{:S(2)}, u32[]{:S(2)}) async-start(bf16[32,1,64,256]{3,2,1,0:T(8,128)(2,1)} %broadcast_in_dim.67), calls=%async_computation | async-start | bytes 2097152 | tf_op jit(solution)/shard_map/all_to_all | solution.py:23
  12.4 14.0 %all-to-all-done = bf16[32,1,64,256]{3,2,1,0:T(8,128)(2,1)S(1)} async-done(((bf16[32,1,64,256]{3,2,1,0:T(8,128)(2,1)}), bf16[32,1,64,256]{3,2,1,0:T(8,128)(2,1)S(1)}, u32[]{:S(2)}, u32[]{:S(2)}) %all-to-all-start) | async-done | bytes 1048608 | tf_op jit(solution)/shard_map/all_to_all | solution.py:23
  26.9 1.9 fusion.10
  30.6 14.8 %collective-permute-start.1 = (bf16[64,256]{1,0:T(8,128)(2,1)S(1)}, bf16[64,256]{1,0:T(8,128)(2,1)S(1)}, u32[]{:S(2)}, u32[]{:S(2)}) collective-permute-start(bf16[64,256]{1,0:T(8,128)(2,1)S(1)} %convert_element_type.159), channel_id=1, source_target_pairs={{0,256},{32,288},{64,320},{96,352},{128,384},{160,416},{192,448},{... | collective-permute-start | bytes 98312 | tf_op jit(solution)/shard_map/ppermute | solution.py:12
  45.5 2.9 %collective-permute-start.2 = (bf16[64,256]{1,0:T(8,128)(2,1)S(1)}, bf16[64,256]{1,0:T(8,128)(2,1)S(1)}, u32[]{:S(2)}, u32[]{:S(2)}) collective-permute-start(bf16[64,256]{1,0:T(8,128)(2,1)S(1)} %convert_element_type.161), channel_id=1, source_target_pairs={{0,480},{32,0},{64,32},{96,64},{128,96},{160,128},{192,160},{224,1... | collective-permute-start | bytes 98312 | tf_op jit(solution)/shard_map/ppermute | solution.py:12
  48.4 2.9 %collective-permute-start = (bf16[64,256]{1,0:T(8,128)(2,1)S(1)}, bf16[64,256]{1,0:T(8,128)(2,1)S(1)}, u32[]{:S(2)}, u32[]{:S(2)}) collective-permute-start(bf16[64,256]{1,0:T(8,128)(2,1)S(1)} %convert_element_type.157), channel_id=1, source_target_pairs={{0,32},{32,64},{64,96},{96,128},{128,160},{160,192},{192,224},{224... | collective-permute-start | bytes 98312 | tf_op jit(solution)/shard_map/ppermute | solution.py:12
  51.6 2.6 %collective-permute-done = bf16[64,256]{1,0:T(8,128)(2,1)S(1)} collective-permute-done((bf16[64,256]{1,0:T(8,128)(2,1)S(1)}, bf16[64,256]{1,0:T(8,128)(2,1)S(1)}, u32[]{:S(2)}, u32[]{:S(2)}) %collective-permute-start) | collective-permute-done | bytes 32800 | tf_op jit(solution)/shard_map/ppermute | solution.py:12
  55.5 4.1 %all-to-all-start.1 = ((bf16[32,1,64,256]{3,2,1,0:T(8,128)(2,1)}), bf16[32,1,64,256]{3,2,1,0:T(8,128)(2,1)S(1)}, u32[]{:S(2)}, u32[]{:S(2)}) async-start(bf16[32,1,64,256]{3,2,1,0:T(8,128)(2,1)} %broadcast_in_dim.68), calls=%async_computation.1 | async-start | bytes 2097152 | tf_op jit(solution)/shard_map/all_to_all | solution.py:23
  60.2 1.8 fusion.6
  62.9 13.5 %all-to-all-done.1 = bf16[32,1,64,256]{3,2,1,0:T(8,128)(2,1)S(1)} async-done(((bf16[32,1,64,256]{3,2,1,0:T(8,128)(2,1)}), bf16[32,1,64,256]{3,2,1,0:T(8,128)(2,1)S(1)}, u32[]{:S(2)}, u32[]{:S(2)}) %all-to-all-start.1) | async-done | bytes 1048608 | tf_op jit(solution)/shard_map/all_to_all | solution.py:23
  79.9 6.3 %collective-permute-start.4 = (bf16[64,256]{1,0:T(8,128)(2,1)S(1)}, bf16[64,256]{1,0:T(8,128)(2,1)S(1)}, u32[]{:S(2)}, u32[]{:S(2)}) collective-permute-start(bf16[64,256]{1,0:T(8,128)(2,1)S(1)} %bitcast.224), channel_id=1, source_target_pairs={{0,256},{32,288},{64,320},{96,352},{128,384},{160,416},{192,448},{... | collective-permute-start | bytes 98312 | tf_op jit(solution)/shard_map/ppermute | solution.py:12
  86.2 5.1 %collective-permute-start.5 = (bf16[64,256]{1,0:T(8,128)(2,1)S(1)}, bf16[64,256]{1,0:T(8,128)(2,1)S(1)}, u32[]{:S(2)}, u32[]{:S(2)}) collective-permute-start(bf16[64,256]{1,0:T(8,128)(2,1)S(1)} %bitcast.223), channel_id=1, source_target_pairs={{0,480},{32,0},{64,32},{96,64},{128,96},{160,128},{192,160},{224,1... | collective-permute-start | bytes 98312 | tf_op jit(solution)/shard_map/ppermute | solution.py:12
  91.3 1.9 collective-permute-start.3
  94.4 2.7 %collective-permute-done.3 = bf16[64,256]{1,0:T(8,128)(2,1)S(1)} collective-permute-done((bf16[64,256]{1,0:T(8,128)(2,1)S(1)}, bf16[64,256]{1,0:T(8,128)(2,1)S(1)}, u32[]{:S(2)}, u32[]{:S(2)}) %collective-permute-start.3) | collective-permute-done | bytes 32800 | tf_op jit(solution)/shard_map/ppermute | solution.py:12
  97.5 30.1 %all-gather = bf16[1024,256]{1,0:T(8,128)(2,1)S(1)} all-gather(bf16[64,256]{1,0:T(8,128)(2,1)S(1)} %get-tuple-element.50), channel_id=2, replica_groups=mesh['row'=16,'col'=32] {'row'}, dimensions={0}, use_global_device_ids=true | all-gather | bytes 557056 | tf_op jit(solution)/shard_map/all_gather | solution.py:143
  134.0 3.4 %collective-permute-start.7 = (bf16[64,256]{1,0:T(8,128)(2,1)S(1)}, bf16[64,256]{1,0:T(8,128)(2,1)S(1)}, u32[]{:S(2)}, u32[]{:S(2)}) collective-permute-start(bf16[64,256]{1,0:T(8,128)(2,1)S(1)} %convert_element_type.180), channel_id=1, source_target_pairs={{0,16},{1,17},{2,18},{3,19},{4,20},{5,21},{6,22},{7,23},{8,24},{9,... | collective-permute-start | bytes 98312 | tf_op jit(solution)/shard_map/ppermute | solution.py:12
  137.4 1.9 collective-permute-start.8
  139.3 2.4 %collective-permute-start.6 = (bf16[64,256]{1,0:T(8,128)(2,1)S(1)}, bf16[64,256]{1,0:T(8,128)(2,1)S(1)}, u32[]{:S(2)}, u32[]{:S(2)}) collective-permute-start(bf16[64,256]{1,0:T(8,128)(2,1)S(1)} %convert_element_type.178), channel_id=1, source_target_pairs={{0,1},{1,2},{2,3},{3,4},{4,5},{5,6},{6,7},{7,8},{8,9},{9,10},{10,1... | collective-permute-start | bytes 98312 | tf_op jit(solution)/shard_map/ppermute | solution.py:12
  142.8 5.1 %collective-permute-done.6 = bf16[64,256]{1,0:T(8,128)(2,1)S(1)} collective-permute-done((bf16[64,256]{1,0:T(8,128)(2,1)S(1)}, bf16[64,256]{1,0:T(8,128)(2,1)S(1)}, u32[]{:S(2)}, u32[]{:S(2)}) %collective-permute-start.6) | collective-permute-done | bytes 32800 | tf_op jit(solution)/shard_map/ppermute | solution.py:12
  148.0 30.0 %all-gather.1 = bf16[1024,256]{1,0:T(8,128)(2,1)S(1)} all-gather(bf16[64,256]{1,0:T(8,128)(2,1)S(1)} %get-tuple-element.52), channel_id=3, replica_groups=mesh['row'=16,'col'=32] {'row'}, dimensions={0}, use_global_device_ids=true | all-gather | bytes 557056 | tf_op jit(solution)/shard_map/all_gather | solution.py:143
  181.3 1.9 collective-permute-start.9
  183.2 7.0 %collective-permute-start.11 = (bf16[64,256]{1,0:T(8,128)(2,1)S(1)}, bf16[64,256]{1,0:T(8,128)(2,1)S(1)}, u32[]{:S(2)}, u32[]{:S(2)}) collective-permute-start(bf16[64,256]{1,0:T(8,128)(2,1)S(1)} %get-tuple-element.26), channel_id=1, source_target_pairs={{0,31},{1,0},{2,1},{3,2},{4,3},{5,4},{6,5},{7,6},{8,7},{9,8},{10,9... | collective-permute-start | bytes 98312 | tf_op jit(solution)/shard_map/ppermute | solution.py:12
  190.2 1.9 collective-permute-start.10
  192.2 5.4 %collective-permute-done.10 = bf16[64,256]{1,0:T(8,128)(2,1)S(1)} collective-permute-done((bf16[64,256]{1,0:T(8,128)(2,1)S(1)}, bf16[64,256]{1,0:T(8,128)(2,1)S(1)}, u32[]{:S(2)}, u32[]{:S(2)}) %collective-permute-start.10) | collective-permute-done | bytes 32800 | tf_op jit(solution)/shard_map/ppermute | solution.py:12
  (74 shorter events, 26.9 us)
Async XLA Ops:
  2.2 24.1 %all-to-all-start = ((bf16[32,1,64,256]{3,2,1,0:T(8,128)(2,1)}), bf16[32,1,64,256]{3,2,1,0:T(8,128)(2,1)S(1)}, u32[]{:S(2)}, u32[]{:S(2)}) async-start(bf16[32,1,64,256]{3,2,1,0:T(8,128)(2,1)} %broadcast_in_dim.67), calls=%async_computation | async-start | bytes 2097152 | tf_op jit(solution)/shard_map/all_to_all | solution.py:23
  26.9 27.3 %copy-start = (bf16[3,1,1,256,256]{4,3,2,1,0:T(8,128)(2,1)S(1)}, bf16[3,1,1,256,256]{4,3,2,1,0:T(8,128)(2,1)}, u32[]{:S(2)}) copy-start(bf16[3,1,1,256,256]{4,3,2,1,0:T(8,128)(2,1)} %param.10) | copy-start | bytes 1179652
  26.9 27.3 %copy-start.1 = (f32[3,1,1,64,256]{4,3,2,1,0:T(8,128)S(1)}, f32[3,1,1,64,256]{4,3,2,1,0:T(8,128)}, u32[]{:S(2)}) copy-start(f32[3,1,1,64,256]{4,3,2,1,0:T(8,128)} %param.9) | copy-start | bytes 589828
  30.6 20.9 %collective-permute-start.1 = (bf16[64,256]{1,0:T(8,128)(2,1)S(1)}, bf16[64,256]{1,0:T(8,128)(2,1)S(1)}, u32[]{:S(2)}, u32[]{:S(2)}) collective-permute-start(bf16[64,256]{1,0:T(8,128)(2,1)S(1)} %convert_element_type.159), channel_id=1, source_target_pairs={{0,256},{32,288},{64,320},{96,352},{128,384},{160,416},{192,448},{... | collective-permute-start | bytes 98312 | tf_op jit(solution)/shard_map/ppermute | solution.py:12
  45.5 6.1 %collective-permute-start.2 = (bf16[64,256]{1,0:T(8,128)(2,1)S(1)}, bf16[64,256]{1,0:T(8,128)(2,1)S(1)}, u32[]{:S(2)}, u32[]{:S(2)}) collective-permute-start(bf16[64,256]{1,0:T(8,128)(2,1)S(1)} %convert_element_type.161), channel_id=1, source_target_pairs={{0,480},{32,0},{64,32},{96,64},{128,96},{160,128},{192,160},{224,1... | collective-permute-start | bytes 98312 | tf_op jit(solution)/shard_map/ppermute | solution.py:12
  48.4 5.8 %collective-permute-start = (bf16[64,256]{1,0:T(8,128)(2,1)S(1)}, bf16[64,256]{1,0:T(8,128)(2,1)S(1)}, u32[]{:S(2)}, u32[]{:S(2)}) collective-permute-start(bf16[64,256]{1,0:T(8,128)(2,1)S(1)} %convert_element_type.157), channel_id=1, source_target_pairs={{0,32},{32,64},{64,96},{96,128},{128,160},{160,192},{192,224},{224... | collective-permute-start | bytes 98312 | tf_op jit(solution)/shard_map/ppermute | solution.py:12
  55.5 20.8 %all-to-all-start.1 = ((bf16[32,1,64,256]{3,2,1,0:T(8,128)(2,1)}), bf16[32,1,64,256]{3,2,1,0:T(8,128)(2,1)S(1)}, u32[]{:S(2)}, u32[]{:S(2)}) async-start(bf16[32,1,64,256]{3,2,1,0:T(8,128)(2,1)} %broadcast_in_dim.68), calls=%async_computation.1 | async-start | bytes 2097152 | tf_op jit(solution)/shard_map/all_to_all | solution.py:23
  79.9 14.5 %collective-permute-start.4 = (bf16[64,256]{1,0:T(8,128)(2,1)S(1)}, bf16[64,256]{1,0:T(8,128)(2,1)S(1)}, u32[]{:S(2)}, u32[]{:S(2)}) collective-permute-start(bf16[64,256]{1,0:T(8,128)(2,1)S(1)} %bitcast.224), channel_id=1, source_target_pairs={{0,256},{32,288},{64,320},{96,352},{128,384},{160,416},{192,448},{... | collective-permute-start | bytes 98312 | tf_op jit(solution)/shard_map/ppermute | solution.py:12
  86.2 8.2 %collective-permute-start.5 = (bf16[64,256]{1,0:T(8,128)(2,1)S(1)}, bf16[64,256]{1,0:T(8,128)(2,1)S(1)}, u32[]{:S(2)}, u32[]{:S(2)}) collective-permute-start(bf16[64,256]{1,0:T(8,128)(2,1)S(1)} %bitcast.223), channel_id=1, source_target_pairs={{0,480},{32,0},{64,32},{96,64},{128,96},{160,128},{192,160},{224,1... | collective-permute-start | bytes 98312 | tf_op jit(solution)/shard_map/ppermute | solution.py:12
  91.3 5.8 %collective-permute-start.3 = (bf16[64,256]{1,0:T(8,128)(2,1)S(1)}, bf16[64,256]{1,0:T(8,128)(2,1)S(1)}, u32[]{:S(2)}, u32[]{:S(2)}) collective-permute-start(bf16[64,256]{1,0:T(8,128)(2,1)S(1)} %bitcast.222), channel_id=1, source_target_pairs={{0,32},{32,64},{64,96},{96,128},{128,160},{160,192},{192,224},{224... | collective-permute-start | bytes 98312 | tf_op jit(solution)/shard_map/ppermute | solution.py:12
  134.0 8.8 %collective-permute-start.7 = (bf16[64,256]{1,0:T(8,128)(2,1)S(1)}, bf16[64,256]{1,0:T(8,128)(2,1)S(1)}, u32[]{:S(2)}, u32[]{:S(2)}) collective-permute-start(bf16[64,256]{1,0:T(8,128)(2,1)S(1)} %convert_element_type.180), channel_id=1, source_target_pairs={{0,16},{1,17},{2,18},{3,19},{4,20},{5,21},{6,22},{7,23},{8,24},{9,... | collective-permute-start | bytes 98312 | tf_op jit(solution)/shard_map/ppermute | solution.py:12
  137.4 5.4 %collective-permute-start.8 = (bf16[64,256]{1,0:T(8,128)(2,1)S(1)}, bf16[64,256]{1,0:T(8,128)(2,1)S(1)}, u32[]{:S(2)}, u32[]{:S(2)}) collective-permute-start(bf16[64,256]{1,0:T(8,128)(2,1)S(1)} %convert_element_type.182), channel_id=1, source_target_pairs={{0,31},{1,0},{2,1},{3,2},{4,3},{5,4},{6,5},{7,6},{8,7},{9,8},{10,9... | collective-permute-start | bytes 98312 | tf_op jit(solution)/shard_map/ppermute | solution.py:12
  139.3 8.6 %collective-permute-start.6 = (bf16[64,256]{1,0:T(8,128)(2,1)S(1)}, bf16[64,256]{1,0:T(8,128)(2,1)S(1)}, u32[]{:S(2)}, u32[]{:S(2)}) collective-permute-start(bf16[64,256]{1,0:T(8,128)(2,1)S(1)} %convert_element_type.178), channel_id=1, source_target_pairs={{0,1},{1,2},{2,3},{3,4},{4,5},{5,6},{6,7},{7,8},{8,9},{9,10},{10,1... | collective-permute-start | bytes 98312 | tf_op jit(solution)/shard_map/ppermute | solution.py:12
  181.3 10.8 %collective-permute-start.9 = (bf16[64,256]{1,0:T(8,128)(2,1)S(1)}, bf16[64,256]{1,0:T(8,128)(2,1)S(1)}, u32[]{:S(2)}, u32[]{:S(2)}) collective-permute-start(bf16[64,256]{1,0:T(8,128)(2,1)S(1)} %get-tuple-element.25), channel_id=1, source_target_pairs={{0,1},{1,2},{2,3},{3,4},{4,5},{5,6},{6,7},{7,8},{8,9},{9,10},{10,1... | collective-permute-start | bytes 98312 | tf_op jit(solution)/shard_map/ppermute | solution.py:12
  183.2 8.9 %collective-permute-start.11 = (bf16[64,256]{1,0:T(8,128)(2,1)S(1)}, bf16[64,256]{1,0:T(8,128)(2,1)S(1)}, u32[]{:S(2)}, u32[]{:S(2)}) collective-permute-start(bf16[64,256]{1,0:T(8,128)(2,1)S(1)} %get-tuple-element.26), channel_id=1, source_target_pairs={{0,31},{1,0},{2,1},{3,2},{4,3},{5,4},{6,5},{7,6},{8,7},{9,8},{10,9... | collective-permute-start | bytes 98312 | tf_op jit(solution)/shard_map/ppermute | solution.py:12
  190.2 7.3 %collective-permute-start.10 = (bf16[64,256]{1,0:T(8,128)(2,1)S(1)}, bf16[64,256]{1,0:T(8,128)(2,1)S(1)}, u32[]{:S(2)}, u32[]{:S(2)}) collective-permute-start(bf16[64,256]{1,0:T(8,128)(2,1)S(1)} %get-tuple-element.27), channel_id=1, source_target_pairs={{0,16},{1,17},{2,18},{3,19},{4,20},{5,21},{6,22},{7,23},{8,24},{9,... | collective-permute-start | bytes 98312 | tf_op jit(solution)/shard_map/ppermute | solution.py:12
where the time goes:
time: 199 us; the launch traced here: 198 us
  starting transfers between devices  63.9 us (32%)
  blocking collectives  60.1 us (30%)
  waiting for transfers between devices  44.4 us (22%)
  matrix products  16.8 us (8%)
  local copies, waits for them, and re-layouts  8.54 us (4%)
  other arithmetic  4.13 us (2%)
    all_gather x2, blocking collectives, shards(): gathered_back[current] = lax.all_gather(outgoing, 'row', axis=0, tiled=True)  60.1 us
    ppermute x12, starting transfers between devices, from_behind(): return lax.ppermute(value, axis, pairs)  52.6 us
    all_to_all x2, waiting for transfers between devices, from_everyone(): lax.all_to_all(jnp.broadcast_to(value[None], (count, *value.shape)), axis...  27.4 us
    ppermute x12, waiting for transfers between devices, from_behind(): return lax.ppermute(value, axis, pairs)  17 us
    all_to_all x2, starting transfers between devices, from_everyone(): lax.all_to_all(jnp.broadcast_to(value[None], (count, *value.shape)), axis...  11.4 us
    dot_general x3, matrix products, shards(): jnp.einsum('snb,sab->sna', picked, blocks[pair_idx], preferred_element_ty...  5.58 us
    dot_general x3, matrix products, shards(): jnp.einsum('snb,sba->sna', picked, blocks[pair_idx], preferred_element_ty...  5.14 us
    dot_general x6, matrix products, spread_rows(): jnp.dot(onehot, flattened, precision=lax.Precision.HIGHEST, preferred_ele...  4.19 us
  transfers between devices with their start and end apart: 14, of which 7 were waited for; matrix products, arithmetic and copies ran while one was open for 4% of the time, Pallas kernels for 0%

commit v1 on v0

--- a/solution.py
+++ b/solution.py
@@ -140,7 +140,35 @@
         solutions[current] = answer
         if current > 0:
             outgoing = answer.astype(jnp.bfloat16)[None]
-            gathered_back[current] = lax.all_gather(outgoing, "row", axis=0, tiled=True)
+
+            def _note_ladders(buf):
+                which_axis = "row"
+                row_out = jax.lax.axis_size(which_axis)
+                arr_next = jax.lax.axis_index(which_axis)
+                later, v_next, tmp = (row_out, arr_next, buf.shape[0])
+                all_rows = []
+                for p in range(later):
+                    all_rows.append((p, (p + 1) % later))
+                vals = []
+                for p in range(later):
+                    vals.append((p, (p - 1) % later))
+                found_now = jnp.zeros((*buf.shape[:0], later * tmp, *buf.shape[1:]), buf.dtype)
+                found_now = lax.dynamic_update_slice_in_dim(found_now, buf, v_next * tmp, axis=0)
+                side_arr = mat_out = buf
+                z_new = later // 2
+                for to_i in range(1, z_new + 1):
+                    side_arr = jax.lax.ppermute(side_arr, which_axis, all_rows)
+                    found_now = lax.dynamic_update_slice_in_dim(
+                        found_now, side_arr, (v_next - to_i) % later * tmp, axis=0
+                    )
+                    if to_i < later - z_new:
+                        mat_out = jax.lax.ppermute(mat_out, which_axis, vals)
+                        found_now = lax.dynamic_update_slice_in_dim(
+                            found_now, mat_out, (v_next + to_i) % later * tmp, axis=0
+                        )
+                return found_now
+
+            gathered_back[current] = _note_ladders(outgoing)
     return jnp.stack(solutions)[:, None, None]
 
 

time: 199 us -> 251 us (1.26)
  the two profiles are of different devices: /device:TPU:32 before, /device:TPU:4 now
where the time goes in v1:
time: 251 us; the launch traced here: 249 us
  starting transfers between devices  168 us (67%)
  waiting for transfers between devices  50.7 us (20%)
  matrix products  16.8 us (7%)
  local copies, waits for them, and re-layouts  8.94 us (4%)
  other arithmetic  3.46 us (1%)
    ppermute x14, starting transfers between devices, _note_ladders(): mat_out = jax.lax.ppermute(mat_out, which_axis, vals)  70.8 us
    ppermute x12, starting transfers between devices, from_behind(): return lax.ppermute(value, axis, pairs)  49.6 us
    ppermute x16, starting transfers between devices, _note_ladders(): side_arr = jax.lax.ppermute(side_arr, which_axis, all_rows)  32 us
    all_to_all x2, waiting for transfers between devices, from_everyone(): lax.all_to_all(jnp.broadcast_to(value[None], (count, *value.shape)), axis...  24.1 us
    ppermute x12, waiting for transfers between devices, from_behind(): return lax.ppermute(value, axis, pairs)  16.4 us
    all_to_all x2, starting transfers between devices, from_everyone(): lax.all_to_all(jnp.broadcast_to(value[None], (count, *value.shape)), axis...  15.4 us
    ppermute x16, waiting for transfers between devices, _note_ladders(): side_arr = jax.lax.ppermute(side_arr, which_axis, all_rows)  10.2 us
    dot_general x3, matrix products, shards(): jnp.einsum('snb,sab->sna', picked, blocks[pair_idx], preferred_element_ty...  5.58 us
  transfers between devices with their start and end apart: 44, of which 9 were waited for; matrix products, arithmetic and copies ran while one was open for 4% of the time, Pallas kernels for 0%

profile of v1, /device:TPU:4, one launch (start us, length us, event | category | flops | bytes accessed | tf_op | source)
XLA Modules:
  0.0 249.2 jit_solution(14433370067061118764)
XLA Ops:
  2.2 9.5 %all-to-all-start = ((bf16[32,1,64,256]{3,2,1,0:T(8,128)(2,1)}), bf16[32,1,64,256]{3,2,1,0:T(8,128)(2,1)S(1)}, u32[]{:S(2)}, u32[]{:S(2)}) async-start(bf16[32,1,64,256]{3,2,1,0:T(8,128)(2,1)} %broadcast_in_dim.67), calls=%async_computation | async-start | bytes 2097152 | tf_op jit(solution)/shard_map/all_to_all | solution.py:23
  13.9 12.7 %all-to-all-done = bf16[32,1,64,256]{3,2,1,0:T(8,128)(2,1)S(1)} async-done(((bf16[32,1,64,256]{3,2,1,0:T(8,128)(2,1)}), bf16[32,1,64,256]{3,2,1,0:T(8,128)(2,1)S(1)}, u32[]{:S(2)}, u32[]{:S(2)}) %all-to-all-start) | async-done | bytes 1048608 | tf_op jit(solution)/shard_map/all_to_all | solution.py:23
  30.8 9.5 %collective-permute-start.2 = (bf16[64,256]{1,0:T(8,128)(2,1)S(1)}, bf16[64,256]{1,0:T(8,128)(2,1)S(1)}, u32[]{:S(2)}, u32[]{:S(2)}) collective-permute-start(bf16[64,256]{1,0:T(8,128)(2,1)S(1)} %convert_element_type.161), channel_id=1, source_target_pairs={{0,480},{32,0},{64,32},{96,64},{128,96},{160,128},{192,160},{224,1... | collective-permute-start | bytes 98312 | tf_op jit(solution)/shard_map/ppermute | solution.py:12
  40.4 6.3 %collective-permute-start.1 = (bf16[64,256]{1,0:T(8,128)(2,1)S(1)}, bf16[64,256]{1,0:T(8,128)(2,1)S(1)}, u32[]{:S(2)}, u32[]{:S(2)}) collective-permute-start(bf16[64,256]{1,0:T(8,128)(2,1)S(1)} %convert_element_type.159), channel_id=1, source_target_pairs={{0,256},{32,288},{64,320},{96,352},{128,384},{160,416},{192,448},{... | collective-permute-start | bytes 98312 | tf_op jit(solution)/shard_map/ppermute | solution.py:12
  50.8 4.4 %collective-permute-done.1 = bf16[64,256]{1,0:T(8,128)(2,1)S(1)} collective-permute-done((bf16[64,256]{1,0:T(8,128)(2,1)S(1)}, bf16[64,256]{1,0:T(8,128)(2,1)S(1)}, u32[]{:S(2)}, u32[]{:S(2)}) %collective-permute-start.1) | collective-permute-done | bytes 32800 | tf_op jit(solution)/shard_map/ppermute | solution.py:12
  56.6 5.8 %all-to-all-start.1 = ((bf16[32,1,64,256]{3,2,1,0:T(8,128)(2,1)}), bf16[32,1,64,256]{3,2,1,0:T(8,128)(2,1)S(1)}, u32[]{:S(2)}, u32[]{:S(2)}) async-start(bf16[32,1,64,256]{3,2,1,0:T(8,128)(2,1)} %broadcast_in_dim.68), calls=%async_computation.1 | async-start | bytes 2097152 | tf_op jit(solution)/shard_map/all_to_all | solution.py:23
  65.8 11.4 %all-to-all-done.1 = bf16[32,1,64,256]{3,2,1,0:T(8,128)(2,1)S(1)} async-done(((bf16[32,1,64,256]{3,2,1,0:T(8,128)(2,1)}), bf16[32,1,64,256]{3,2,1,0:T(8,128)(2,1)S(1)}, u32[]{:S(2)}, u32[]{:S(2)}) %all-to-all-start.1) | async-done | bytes 1048608 | tf_op jit(solution)/shard_map/all_to_all | solution.py:23
  83.5 6.9 %collective-permute-start.4 = (bf16[64,256]{1,0:T(8,128)(2,1)S(1)}, bf16[64,256]{1,0:T(8,128)(2,1)S(1)}, u32[]{:S(2)}, u32[]{:S(2)}) collective-permute-start(bf16[64,256]{1,0:T(8,128)(2,1)S(1)} %bitcast.214), channel_id=1, source_target_pairs={{0,256},{32,288},{64,320},{96,352},{128,384},{160,416},{192,448},{... | collective-permute-start | bytes 98312 | tf_op jit(solution)/shard_map/ppermute | solution.py:12
  107.8 5.1 %collective-permute-start.9 = (bf16[1,64,256]{2,1,0:T(8,128)(2,1)S(1)}, bf16[1,64,256]{2,1,0:T(8,128)(2,1)S(1)}, u32[]{:S(2)}, u32[]{:S(2)}) collective-permute-start(bf16[1,64,256]{2,1,0:T(8,128)(2,1)S(1)} %collective-permute-done.7), channel_id=1, source_target_pairs={{0,480},{32,0},{64,32},{96,64},{128,96},{160,128},{192,160},{224,1... | collective-permute-start | bytes 98312 | tf_op jit(solution)/shard_map/ppermute | solution.py:165
  115.0 5.1 %collective-permute-start.11 = (bf16[1,64,256]{2,1,0:T(8,128)(2,1)S(1)}, bf16[1,64,256]{2,1,0:T(8,128)(2,1)S(1)}, u32[]{:S(2)}, u32[]{:S(2)}) collective-permute-start(bf16[1,64,256]{2,1,0:T(8,128)(2,1)S(1)} %collective-permute-done.9), channel_id=1, source_target_pairs={{0,480},{32,0},{64,32},{96,64},{128,96},{160,128},{192,160},{224,1... | collective-permute-start | bytes 98312 | tf_op jit(solution)/shard_map/ppermute | solution.py:165
  122.1 5.1 %collective-permute-start.13 = (bf16[1,64,256]{2,1,0:T(8,128)(2,1)S(1)}, bf16[1,64,256]{2,1,0:T(8,128)(2,1)S(1)}, u32[]{:S(2)}, u32[]{:S(2)}) collective-permute-start(bf16[1,64,256]{2,1,0:T(8,128)(2,1)S(1)} %collective-permute-done.11), channel_id=1, source_target_pairs={{0,480},{32,0},{64,32},{96,64},{128,96},{160,128},{192,160},{224,1... | collective-permute-start | bytes 98312 | tf_op jit(solution)/shard_map/ppermute | solution.py:165
  129.2 5.1 %collective-permute-start.15 = (bf16[1,64,256]{2,1,0:T(8,128)(2,1)S(1)}, bf16[1,64,256]{2,1,0:T(8,128)(2,1)S(1)}, u32[]{:S(2)}, u32[]{:S(2)}) collective-permute-start(bf16[1,64,256]{2,1,0:T(8,128)(2,1)S(1)} %collective-permute-done.13), channel_id=1, source_target_pairs={{0,480},{32,0},{64,32},{96,64},{128,96},{160,128},{192,160},{224,1... | collective-permute-start | bytes 98312 | tf_op jit(solution)/shard_map/ppermute | solution.py:165
  136.3 5.1 %collective-permute-start.17 = (bf16[1,64,256]{2,1,0:T(8,128)(2,1)S(1)}, bf16[1,64,256]{2,1,0:T(8,128)(2,1)S(1)}, u32[]{:S(2)}, u32[]{:S(2)}) collective-permute-start(bf16[1,64,256]{2,1,0:T(8,128)(2,1)S(1)} %collective-permute-done.15), channel_id=1, source_target_pairs={{0,480},{32,0},{64,32},{96,64},{128,96},{160,128},{192,160},{224,1... | collective-permute-start | bytes 98312 | tf_op jit(solution)/shard_map/ppermute | solution.py:165
  143.5 5.1 %collective-permute-start.19 = (bf16[1,64,256]{2,1,0:T(8,128)(2,1)S(1)}, bf16[1,64,256]{2,1,0:T(8,128)(2,1)S(1)}, u32[]{:S(2)}, u32[]{:S(2)}) collective-permute-start(bf16[1,64,256]{2,1,0:T(8,128)(2,1)S(1)} %collective-permute-done.17), channel_id=1, source_target_pairs={{0,480},{32,0},{64,32},{96,64},{128,96},{160,128},{192,160},{224,1... | collective-permute-start | bytes 98312 | tf_op jit(solution)/shard_map/ppermute | solution.py:165
  150.6 5.0 %collective-permute-done.20 = bf16[1,64,256]{2,1,0:T(8,128)(2,1)S(1)} collective-permute-done((bf16[1,64,256]{2,1,0:T(8,128)(2,1)S(1)}, bf16[1,64,256]{2,1,0:T(8,128)(2,1)S(1)}, u32[]{:S(2)}, u32[]{:S(2)}) %collective-permute-start.20) | collective-permute-done | bytes 32800 | tf_op jit(solution)/shard_map/ppermute | solution.py:160
  161.7 4.4 %collective-permute-start.22 = (bf16[64,256]{1,0:T(8,128)(2,1)S(1)}, bf16[64,256]{1,0:T(8,128)(2,1)S(1)}, u32[]{:S(2)}, u32[]{:S(2)}) collective-permute-start(bf16[64,256]{1,0:T(8,128)(2,1)S(1)} %convert_element_type.180), channel_id=1, source_target_pairs={{0,16},{1,17},{2,18},{3,19},{4,20},{5,21},{6,22},{7,23},{8,24},{9,... | collective-permute-start | bytes 98312 | tf_op jit(solution)/shard_map/ppermute | solution.py:12
  176.6 5.1 %collective-permute-start.25 = (bf16[1,64,256]{2,1,0:T(8,128)(2,1)S(1)}, bf16[1,64,256]{2,1,0:T(8,128)(2,1)S(1)}, u32[]{:S(2)}, u32[]{:S(2)}) collective-permute-start(bf16[1,64,256]{2,1,0:T(8,128)(2,1)S(1)} %get-tuple-element.16), channel_id=1, source_target_pairs={{0,480},{32,0},{64,32},{96,64},{128,96},{160,128},{192,160},{224,1... | collective-permute-start | bytes 98312 | tf_op jit(solution)/shard_map/ppermute | solution.py:165
  183.7 5.1 %collective-permute-start.27 = (bf16[1,64,256]{2,1,0:T(8,128)(2,1)S(1)}, bf16[1,64,256]{2,1,0:T(8,128)(2,1)S(1)}, u32[]{:S(2)}, u32[]{:S(2)}) collective-permute-start(bf16[1,64,256]{2,1,0:T(8,128)(2,1)S(1)} %collective-permute-done.25), channel_id=1, source_target_pairs={{0,480},{32,0},{64,32},{96,64},{128,96},{160,128},{192,160},{224,1... | collective-permute-start | bytes 98312 | tf_op jit(solution)/shard_map/ppermute | solution.py:165
  190.9 5.1 %collective-permute-start.29 = (bf16[1,64,256]{2,1,0:T(8,128)(2,1)S(1)}, bf16[1,64,256]{2,1,0:T(8,128)(2,1)S(1)}, u32[]{:S(2)}, u32[]{:S(2)}) collective-permute-start(bf16[1,64,256]{2,1,0:T(8,128)(2,1)S(1)} %collective-permute-done.27), channel_id=1, source_target_pairs={{0,480},{32,0},{64,32},{96,64},{128,96},{160,128},{192,160},{224,1... | collective-permute-start | bytes 98312 | tf_op jit(solution)/shard_map/ppermute | solution.py:165
  198.0 5.1 %collective-permute-start.31 = (bf16[1,64,256]{2,1,0:T(8,128)(2,1)S(1)}, bf16[1,64,256]{2,1,0:T(8,128)(2,1)S(1)}, u32[]{:S(2)}, u32[]{:S(2)}) collective-permute-start(bf16[1,64,256]{2,1,0:T(8,128)(2,1)S(1)} %collective-permute-done.29), channel_id=1, source_target_pairs={{0,480},{32,0},{64,32},{96,64},{128,96},{160,128},{192,160},{224,1... | collective-permute-start | bytes 98312 | tf_op jit(solution)/shard_map/ppermute | solution.py:165
  205.1 5.1 %collective-permute-start.33 = (bf16[1,64,256]{2,1,0:T(8,128)(2,1)S(1)}, bf16[1,64,256]{2,1,0:T(8,128)(2,1)S(1)}, u32[]{:S(2)}, u32[]{:S(2)}) collective-permute-start(bf16[1,64,256]{2,1,0:T(8,128)(2,1)S(1)} %collective-permute-done.31), channel_id=1, source_target_pairs={{0,480},{32,0},{64,32},{96,64},{128,96},{160,128},{192,160},{224,1... | collective-permute-start | bytes 98312 | tf_op jit(solution)/shard_map/ppermute | solution.py:165
  212.2 5.1 %collective-permute-start.35 = (bf16[1,64,256]{2,1,0:T(8,128)(2,1)S(1)}, bf16[1,64,256]{2,1,0:T(8,128)(2,1)S(1)}, u32[]{:S(2)}, u32[]{:S(2)}) collective-permute-start(bf16[1,64,256]{2,1,0:T(8,128)(2,1)S(1)} %collective-permute-done.33), channel_id=1, source_target_pairs={{0,480},{32,0},{64,32},{96,64},{128,96},{160,128},{192,160},{224,1... | collective-permute-start | bytes 98312 | tf_op jit(solution)/shard_map/ppermute | solution.py:165
  219.4 5.3 %collective-permute-start.37 = (bf16[1,64,256]{2,1,0:T(8,128)(2,1)S(1)}, bf16[1,64,256]{2,1,0:T(8,128)(2,1)S(1)}, u32[]{:S(2)}, u32[]{:S(2)}) collective-permute-start(bf16[1,64,256]{2,1,0:T(8,128)(2,1)S(1)} %collective-permute-done.35), channel_id=1, source_target_pairs={{0,480},{32,0},{64,32},{96,64},{128,96},{160,128},{192,160},{224,1... | collective-permute-start | bytes 98312 | tf_op jit(solution)/shard_map/ppermute | solution.py:165
  226.7 5.0 %collective-permute-done.38 = bf16[1,64,256]{2,1,0:T(8,128)(2,1)S(1)} collective-permute-done((bf16[1,64,256]{2,1,0:T(8,128)(2,1)S(1)}, bf16[1,64,256]{2,1,0:T(8,128)(2,1)S(1)}, u32[]{:S(2)}, u32[]{:S(2)}) %collective-permute-start.38) | collective-permute-done | bytes 32800 | tf_op jit(solution)/shard_map/ppermute | solution.py:160
  (167 shorter events, 99.6 us)
Async XLA Ops:
  2.2 24.3 %all-to-all-start = ((bf16[32,1,64,256]{3,2,1,0:T(8,128)(2,1)}), bf16[32,1,64,256]{3,2,1,0:T(8,128)(2,1)S(1)}, u32[]{:S(2)}, u32[]{:S(2)}) async-start(bf16[32,1,64,256]{3,2,1,0:T(8,128)(2,1)} %broadcast_in_dim.67), calls=%async_computation | async-start | bytes 2097152 | tf_op jit(solution)/shard_map/all_to_all | solution.py:23
  30.8 20.0 %collective-permute-start.2 = (bf16[64,256]{1,0:T(8,128)(2,1)S(1)}, bf16[64,256]{1,0:T(8,128)(2,1)S(1)}, u32[]{:S(2)}, u32[]{:S(2)}) collective-permute-start(bf16[64,256]{1,0:T(8,128)(2,1)S(1)} %convert_element_type.161), channel_id=1, source_target_pairs={{0,480},{32,0},{64,32},{96,64},{128,96},{160,128},{192,160},{224,1... | collective-permute-start | bytes 98312 | tf_op jit(solution)/shard_map/ppermute | solution.py:12
  40.4 14.9 %collective-permute-start.1 = (bf16[64,256]{1,0:T(8,128)(2,1)S(1)}, bf16[64,256]{1,0:T(8,128)(2,1)S(1)}, u32[]{:S(2)}, u32[]{:S(2)}) collective-permute-start(bf16[64,256]{1,0:T(8,128)(2,1)S(1)} %convert_element_type.159), channel_id=1, source_target_pairs={{0,256},{32,288},{64,320},{96,352},{128,384},{160,416},{192,448},{... | collective-permute-start | bytes 98312 | tf_op jit(solution)/shard_map/ppermute | solution.py:12
  46.8 8.5 %collective-permute-start = (bf16[64,256]{1,0:T(8,128)(2,1)S(1)}, bf16[64,256]{1,0:T(8,128)(2,1)S(1)}, u32[]{:S(2)}, u32[]{:S(2)}) collective-permute-start(bf16[64,256]{1,0:T(8,128)(2,1)S(1)} %convert_element_type.157), channel_id=1, source_target_pairs={{0,32},{32,64},{64,96},{96,128},{128,160},{160,192},{192,224},{224... | collective-permute-start | bytes 98312 | tf_op jit(solution)/shard_map/ppermute | solution.py:12
  56.6 20.6 %all-to-all-start.1 = ((bf16[32,1,64,256]{3,2,1,0:T(8,128)(2,1)}), bf16[32,1,64,256]{3,2,1,0:T(8,128)(2,1)S(1)}, u32[]{:S(2)}, u32[]{:S(2)}) async-start(bf16[32,1,64,256]{3,2,1,0:T(8,128)(2,1)} %broadcast_in_dim.68), calls=%async_computation.1 | async-start | bytes 2097152 | tf_op jit(solution)/shard_map/all_to_all | solution.py:23
  80.7 13.3 %collective-permute-start.5 = (bf16[64,256]{1,0:T(8,128)(2,1)S(1)}, bf16[64,256]{1,0:T(8,128)(2,1)S(1)}, u32[]{:S(2)}, u32[]{:S(2)}) collective-permute-start(bf16[64,256]{1,0:T(8,128)(2,1)S(1)} %bitcast.213), channel_id=1, source_target_pairs={{0,480},{32,0},{64,32},{96,64},{128,96},{160,128},{192,160},{224,1... | collective-permute-start | bytes 98312 | tf_op jit(solution)/shard_map/ppermute | solution.py:12
  83.5 14.6 %collective-permute-start.4 = (bf16[64,256]{1,0:T(8,128)(2,1)S(1)}, bf16[64,256]{1,0:T(8,128)(2,1)S(1)}, u32[]{:S(2)}, u32[]{:S(2)}) collective-permute-start(bf16[64,256]{1,0:T(8,128)(2,1)S(1)} %bitcast.214), channel_id=1, source_target_pairs={{0,256},{32,288},{64,320},{96,352},{128,384},{160,416},{192,448},{... | collective-permute-start | bytes 98312 | tf_op jit(solution)/shard_map/ppermute | solution.py:12
  90.5 7.7 %collective-permute-start.3 = (bf16[64,256]{1,0:T(8,128)(2,1)S(1)}, bf16[64,256]{1,0:T(8,128)(2,1)S(1)}, u32[]{:S(2)}, u32[]{:S(2)}) collective-permute-start(bf16[64,256]{1,0:T(8,128)(2,1)S(1)} %bitcast.215), channel_id=1, source_target_pairs={{0,32},{32,64},{64,96},{96,128},{128,160},{160,192},{192,224},{224... | collective-permute-start | bytes 98312 | tf_op jit(solution)/shard_map/ppermute | solution.py:12
  98.5 7.4 %collective-permute-start.6 = (bf16[1,64,256]{2,1,0:T(8,128)(2,1)S(1)}, bf16[1,64,256]{2,1,0:T(8,128)(2,1)S(1)}, u32[]{:S(2)}, u32[]{:S(2)}) collective-permute-start(bf16[1,64,256]{2,1,0:T(8,128)(2,1)S(1)} %get-tuple-element.22), channel_id=1, source_target_pairs={{0,32},{32,64},{64,96},{96,128},{128,160},{160,192},{192,224},{224... | collective-permute-start | bytes 98312 | tf_op jit(solution)/shard_map/ppermute | solution.py:160
  105.9 7.1 %collective-permute-start.8 = (bf16[1,64,256]{2,1,0:T(8,128)(2,1)S(1)}, bf16[1,64,256]{2,1,0:T(8,128)(2,1)S(1)}, u32[]{:S(2)}, u32[]{:S(2)}) collective-permute-start(bf16[1,64,256]{2,1,0:T(8,128)(2,1)S(1)} %collective-permute-done.6), channel_id=1, source_target_pairs={{0,32},{32,64},{64,96},{96,128},{128,160},{160,192},{192,224},{224... | collective-permute-start | bytes 98312 | tf_op jit(solution)/shard_map/ppermute | solution.py:160
  107.8 7.1 %collective-permute-start.9 = (bf16[1,64,256]{2,1,0:T(8,128)(2,1)S(1)}, bf16[1,64,256]{2,1,0:T(8,128)(2,1)S(1)}, u32[]{:S(2)}, u32[]{:S(2)}) collective-permute-start(bf16[1,64,256]{2,1,0:T(8,128)(2,1)S(1)} %collective-permute-done.7), channel_id=1, source_target_pairs={{0,480},{32,0},{64,32},{96,64},{128,96},{160,128},{192,160},{224,1... | collective-permute-start | bytes 98312 | tf_op jit(solution)/shard_map/ppermute | solution.py:165
  113.0 7.1 %collective-permute-start.10 = (bf16[1,64,256]{2,1,0:T(8,128)(2,1)S(1)}, bf16[1,64,256]{2,1,0:T(8,128)(2,1)S(1)}, u32[]{:S(2)}, u32[]{:S(2)}) collective-permute-start(bf16[1,64,256]{2,1,0:T(8,128)(2,1)S(1)} %collective-permute-done.8), channel_id=1, source_target_pairs={{0,32},{32,64},{64,96},{96,128},{128,160},{160,192},{192,224},{224... | collective-permute-start | bytes 98312 | tf_op jit(solution)/shard_map/ppermute | solution.py:160
  143.5 7.1 %collective-permute-start.19 = (bf16[1,64,256]{2,1,0:T(8,128)(2,1)S(1)}, bf16[1,64,256]{2,1,0:T(8,128)(2,1)S(1)}, u32[]{:S(2)}, u32[]{:S(2)}) collective-permute-start(bf16[1,64,256]{2,1,0:T(8,128)(2,1)S(1)} %collective-permute-done.17), channel_id=1, source_target_pairs={{0,480},{32,0},{64,32},{96,64},{128,96},{160,128},{192,160},{224,1... | collective-permute-start | bytes 98312 | tf_op jit(solution)/shard_map/ppermute | solution.py:165
  159.7 11.1 %collective-permute-start.23 = (bf16[64,256]{1,0:T(8,128)(2,1)S(1)}, bf16[64,256]{1,0:T(8,128)(2,1)S(1)}, u32[]{:S(2)}, u32[]{:S(2)}) collective-permute-start(bf16[64,256]{1,0:T(8,128)(2,1)S(1)} %convert_element_type.182), channel_id=1, source_target_pairs={{0,31},{1,0},{2,1},{3,2},{4,3},{5,4},{6,5},{7,6},{8,7},{9,8},{10,9... | collective-permute-start | bytes 98312 | tf_op jit(solution)/shard_map/ppermute | solution.py:12
  161.7 9.2 %collective-permute-start.22 = (bf16[64,256]{1,0:T(8,128)(2,1)S(1)}, bf16[64,256]{1,0:T(8,128)(2,1)S(1)}, u32[]{:S(2)}, u32[]{:S(2)}) collective-permute-start(bf16[64,256]{1,0:T(8,128)(2,1)S(1)} %convert_element_type.180), channel_id=1, source_target_pairs={{0,16},{1,17},{2,18},{3,19},{4,20},{5,21},{6,22},{7,23},{8,24},{9,... | collective-permute-start | bytes 98312 | tf_op jit(solution)/shard_map/ppermute | solution.py:12
  166.1 7.3 %collective-permute-start.21 = (bf16[64,256]{1,0:T(8,128)(2,1)S(1)}, bf16[64,256]{1,0:T(8,128)(2,1)S(1)}, u32[]{:S(2)}, u32[]{:S(2)}) collective-permute-start(bf16[64,256]{1,0:T(8,128)(2,1)S(1)} %convert_element_type.178), channel_id=1, source_target_pairs={{0,1},{1,2},{2,3},{3,4},{4,5},{5,6},{6,7},{7,8},{8,9},{9,10},{10,1... | collective-permute-start | bytes 98312 | tf_op jit(solution)/shard_map/ppermute | solution.py:12
  173.7 8.1 %collective-permute-start.24 = (bf16[1,64,256]{2,1,0:T(8,128)(2,1)S(1)}, bf16[1,64,256]{2,1,0:T(8,128)(2,1)S(1)}, u32[]{:S(2)}, u32[]{:S(2)}) collective-permute-start(bf16[1,64,256]{2,1,0:T(8,128)(2,1)S(1)} %get-tuple-element.16), channel_id=1, source_target_pairs={{0,32},{32,64},{64,96},{96,128},{128,160},{160,192},{192,224},{224... | collective-permute-start | bytes 98312 | tf_op jit(solution)/shard_map/ppermute | solution.py:160
  210.3 7.2 %collective-permute-start.34 = (bf16[1,64,256]{2,1,0:T(8,128)(2,1)S(1)}, bf16[1,64,256]{2,1,0:T(8,128)(2,1)S(1)}, u32[]{:S(2)}, u32[]{:S(2)}) collective-permute-start(bf16[1,64,256]{2,1,0:T(8,128)(2,1)S(1)} %collective-permute-done.32), channel_id=1, source_target_pairs={{0,32},{32,64},{64,96},{96,128},{128,160},{160,192},{192,224},{224... | collective-permute-start | bytes 98312 | tf_op jit(solution)/shard_map/ppermute | solution.py:160
  212.2 7.1 %collective-permute-start.35 = (bf16[1,64,256]{2,1,0:T(8,128)(2,1)S(1)}, bf16[1,64,256]{2,1,0:T(8,128)(2,1)S(1)}, u32[]{:S(2)}, u32[]{:S(2)}) collective-permute-start(bf16[1,64,256]{2,1,0:T(8,128)(2,1)S(1)} %collective-permute-done.33), channel_id=1, source_target_pairs={{0,480},{32,0},{64,32},{96,64},{128,96},{160,128},{192,160},{224,1... | collective-permute-start | bytes 98312 | tf_op jit(solution)/shard_map/ppermute | solution.py:165
  217.4 7.2 %collective-permute-start.36 = (bf16[1,64,256]{2,1,0:T(8,128)(2,1)S(1)}, bf16[1,64,256]{2,1,0:T(8,128)(2,1)S(1)}, u32[]{:S(2)}, u32[]{:S(2)}) collective-permute-start(bf16[1,64,256]{2,1,0:T(8,128)(2,1)S(1)} %collective-permute-done.34), channel_id=1, source_target_pairs={{0,32},{32,64},{64,96},{96,128},{128,160},{160,192},{192,224},{224... | collective-permute-start | bytes 98312 | tf_op jit(solution)/shard_map/ppermute | solution.py:160
  219.4 7.3 %collective-permute-start.37 = (bf16[1,64,256]{2,1,0:T(8,128)(2,1)S(1)}, bf16[1,64,256]{2,1,0:T(8,128)(2,1)S(1)}, u32[]{:S(2)}, u32[]{:S(2)}) collective-permute-start(bf16[1,64,256]{2,1,0:T(8,128)(2,1)S(1)} %collective-permute-done.35), channel_id=1, source_target_pairs={{0,480},{32,0},{64,32},{96,64},{128,96},{160,128},{192,160},{224,1... | collective-permute-start | bytes 98312 | tf_op jit(solution)/shard_map/ppermute | solution.py:165
  235.0 8.2 %collective-permute-start.41 = (bf16[64,256]{1,0:T(8,128)(2,1)S(1)}, bf16[64,256]{1,0:T(8,128)(2,1)S(1)}, u32[]{:S(2)}, u32[]{:S(2)}) collective-permute-start(bf16[64,256]{1,0:T(8,128)(2,1)S(1)} %get-tuple-element.30), channel_id=1, source_target_pairs={{0,31},{1,0},{2,1},{3,2},{4,3},{5,4},{6,5},{7,6},{8,7},{9,8},{10,9... | collective-permute-start | bytes 98312 | tf_op jit(solution)/shard_map/ppermute | solution.py:12
  236.9 7.3 %collective-permute-start.40 = (bf16[64,256]{1,0:T(8,128)(2,1)S(1)}, bf16[64,256]{1,0:T(8,128)(2,1)S(1)}, u32[]{:S(2)}, u32[]{:S(2)}) collective-permute-start(bf16[64,256]{1,0:T(8,128)(2,1)S(1)} %get-tuple-element.31), channel_id=1, source_target_pairs={{0,16},{1,17},{2,18},{3,19},{4,20},{5,21},{6,22},{7,23},{8,24},{9,... | collective-permute-start | bytes 98312 | tf_op jit(solution)/shard_map/ppermute | solution.py:12
  241.0 7.3 %collective-permute-start.39 = (bf16[64,256]{1,0:T(8,128)(2,1)S(1)}, bf16[64,256]{1,0:T(8,128)(2,1)S(1)}, u32[]{:S(2)}, u32[]{:S(2)}) collective-permute-start(bf16[64,256]{1,0:T(8,128)(2,1)S(1)} %get-tuple-element.29), channel_id=1, source_target_pairs={{0,1},{1,2},{2,3},{3,4},{4,5},{5,6},{6,7},{7,8},{8,9},{9,10},{10,1... | collective-permute-start | bytes 98312 | tf_op jit(solution)/shard_map/ppermute | solution.py:12
  (23 other events, 230.8 us)
